TPU v7x, 32 devices: a whole 2x2x4 slice. The times are simulated.
32 devices in a mesh: groups: 2 (over y), ga: 16 (over z, x, core).
Axes of the slice: x: 2, y: 2, z: 4, core: 2. Of those that a mesh axis runs over, the one named last changes fastest.
Arguments:
- occupied: float32 [2, 1024, 12288], P(None, None, 'ga'), may hold values from -0.0546875 to 0.0546875
- residual: float32 [4, 2, 128, 12288], P('groups', None, None, 'ga'), parts along dimension 0, may hold values from -6 to 6
- old_direction: float32 [4, 2, 128, 12288], P('groups', None, None, 'ga'), parts along dimension 0, may hold values from -6 to 6
- kin_ratio: float32 [12288], P('ga'), may hold values from 0.06 to 5, as said below
- old_dot: float32 [4, 128], P('groups'), parts along dimension 0, may hold values from 6144 to 24576
Outputs:
- direction: float32 [4, 2, 128, 12288], P('groups', None, None, 'ga'), parts along dimension 0
- dot_new: float32 [4, 128], P('groups'), parts along dimension 0
There are 2 independent parts, one for each index of `groups`. A program takes and returns all parts, laid end to end along the dimension named above; an argument that names none is the same for every part. Nothing has to cross between parts.
Inputs may be any that keep to these rules, and one draw needn't show every extreme that they name: `kin_ratio`: positive; grows with the plane-wave index on average and varies from one plane wave to the next.
All inputs are finite; a program needn't handle non-finite values.
Results may differ from a plain program's by a relative error of at most 0.000056.
Values sent between devices are 32-bit elements; how exact they have to be, the bound alone decides.
No kernel may reach another device: no remote copies, remote signals or barrier semaphores. Data moves between devices by JAX's collectives and lax.ppermute only.
A program may use at most 64 MiB of HBM per device.

v0:
```python
import jax
import jax.numpy as jnp
from jax import lax
from jax.sharding import PartitionSpec as P

highest = lax.Precision.HIGHEST


def teter_factor(ratio):
    numerator = 27.0 + 18.0 * ratio + 12.0 * ratio**2 + 8.0 * ratio**3
    return numerator / (numerator + 16.0 * ratio**4)


def margins(occupied, vectors):
    products = jnp.einsum("hng,pcbg->phcnb", occupied, vectors, precision=highest)
    real_part = products[:, 0, 0] + products[:, 1, 1]
    imag_part = products[:, 0, 1] - products[:, 1, 0]
    return jnp.stack([real_part, imag_part], axis=1)


def correction(summed, occ_rows):
    real_part = summed[:, 0]
    imag_part = summed[:, 1]
    coefficient = jnp.stack(
        [jnp.stack([real_part, -imag_part], axis=1), jnp.stack([imag_part, real_part], axis=1)],
        axis=1,
    )
    return jnp.einsum("pchnb,hng->pcbg", coefficient, occ_rows, precision=highest)


def on_device(occupied, residual, old_direction, kin_ratio, old_dot):
    factor = teter_factor(kin_ratio)
    first = margins(occupied, residual)
    first_total = lax.psum(first, "ga")
    gradient = residual - correction(first_total, occupied)
    precond = factor * gradient
    local_dot = jnp.sum(factor * (gradient[:, 0] ** 2 + gradient[:, 1] ** 2), axis=-1)
    second = margins(occupied, precond)
    second_total, dot_new = lax.psum((second, local_dot), "ga")
    projected = precond - correction(second_total, occupied)
    direction = projected + (dot_new / old_dot)[:, None, :, None] * old_direction
    return (direction, dot_new)


def solution(mesh):
    placed = (
        P(None, None, "ga"),
        P("groups", None, None, "ga"),
        P("groups", None, None, "ga"),
        P("ga"),
        P("groups", None),
    )
    return jax.shard_map(
        on_device,
        mesh=mesh,
        in_specs=placed,
        out_specs=(P("groups", None, None, "ga"), P("groups", None)),
        check_vma=False,
    )
```

profile of v0, /device:TPU:0, one launch (start us, length us, event | category | flops | bytes accessed | tf_op | source)
XLA Modules:
  0.0 279.0 jit_solution(1500607859630223277)
XLA Ops:
  7.2 0.0 all-reduce.3.cloned.1.call-start
  7.2 13.1 %fusion.10 = f32[2,2,2,1024,128]{3,4,1,2,0:T(8,128)S(1)} fusion(f32[2,1024,768]{2,1,0:T(8,128)} %param.5, f32[2,2,128,768]{3,2,1,0:T(8,128)} %param.6), kind=kOutput, calls=%fused_computation.12 | convolution fusion | flops 9663676416 | bytes 12058624 | tf_op jit(solution)/shard_map/hng,pcbg->phcnb/dot_general | solution.py:15
  20.4 0.2 fusion.31
  20.5 0.2 fusion.33
  20.7 1.4 pad_maximum_fusion.2
  22.2 0.2 all-reduce.5.cloned.1.call-start
  22.4 0.4 copy-done.3
  22.8 100.4 %all-reduce.3.cloned.1.call-done = f32[2,2,1024,128]{2,3,0,1:T(8,128)} async-done(((f32[2,2,1024,128]{2,3,0,1:T(8,128)}), f32[2,2,1024,128]{2,3,0,1:T(8,128)}) %all-reduce.3.cloned.1.call-update) | async-done | bytes 2097168 | tf_op jit(solution)/shard_map/psum | solution.py:34
  123.2 1.9 slice_negate_fusion.1
  125.2 0.5 maximum_bitcast_fusion
  125.7 0.9 copy-done
  126.6 16.2 %bitcast_subtract_fusion.1 = f32[2,2,128,768]{3,2,1,0:T(8,128)S(1)} fusion(f32[2,2,128,768]{3,2,1,0:T(8,128)S(1)} %copy-done, f32[2,1024,768]{2,1,0:T(8,128)} %param.5, f32[2,1,2,1024,128]{3,4,0,2,1:T(8,128)S(1)} %get-tuple-element.11, f32[2,1,2,1024,128]{3,4,0,2,1:T(8,128)S(1)} %get-tuple-element.10), kind=kOutput, calls=%fused_computation.24 | convolution fusion | flops 9665118208 | bytes 13631488 | tf_op jit(solution)/shard_map/pchnb,hng->pcbg/dot_general | solution.py:28
  142.8 10.2 %fusion.13 = f32[2,2,2,1024,128]{3,4,1,2,0:T(8,128)S(1)} fusion(f32[2,1024,768]{2,1,0:T(8,128)S(1)} %bitcast.84, f32[2,2,128,768]{3,2,1,0:T(8,128)S(1)} %bitcast_subtract_fusion.1, f32[768]{0:T(1024)S(1)} %add_divide_fusion), kind=kOutput, calls=%fused_computation.13 | convolution fusion | flops 9664069632 | bytes 12061696 | tf_op jit(solution)/shard_map/hng,pcbg->phcnb/dot_general | solution.py:15
  153.0 0.2 fusion.28
  153.1 0.2 fusion.30
  153.3 1.4 pad_maximum_fusion.3
  154.7 0.0 all-reduce.5.cloned.1.call-update
  154.8 0.2 fusion.37
  155.0 31.1 %psum.23 = f32[2,128]{1,0:T(2,128)S(1)} all-reduce(f32[2,128]{1,0:T(2,128)S(1)} %fusion.37), channel_id=1, replica_groups=mesh['groups'=2,'ga'=16] {'ga'}, use_global_device_ids=true, to_apply=%region_3.0 | all-reduce | flops 256 | bytes 2048 | tf_op jit(solution)/shard_map/psum | solution.py:39
  186.1 66.3 %all-reduce.5.cloned.1.call-done = f32[2,2,1024,128]{2,3,0,1:T(8,128)} async-done(((f32[2,2,1024,128]{2,3,0,1:T(8,128)}), f32[2,2,1024,128]{2,3,0,1:T(8,128)}) %all-reduce.5.cloned.1.call-update) | async-done | bytes 2097168 | tf_op jit(solution)/shard_map/psum | solution.py:39
  252.5 1.9 slice_negate_fusion
  254.4 0.5 maximum_bitcast_fusion.2
  254.9 0.9 copy-done.1
  255.8 16.4 %fusion.18 = f32[2,2,128,768]{3,2,1,0:T(8,128)} fusion(f32[2,2,128,768]{3,2,1,0:T(8,128)S(1)} %copy-done.1, f32[2,1024,768]{2,1,0:T(8,128)} %param.5, f32[2,2,128,768]{3,2,1,0:T(8,128)S(1)} %bitcast_subtract_fusion.1, f32[2,128]{1,0:T(2,128)S(1)} %div.7, f32[768]{0:T(1024)S(1)} %add_divide_fusion, f32[2,1,2,1024,128]{3,4,0,2,1:T(8,128)S(1)} %get-tuple-element.9, ...), kind=kOutput, calls=%fused_computation.23 | convolution fusion | flops 9666297856 | bytes 15208448 | tf_op jit(solution)/shard_map/pchnb,hng->pcbg/dot_general | solution.py:28
  (15 shorter events, 0.1 us)
Async XLA Ops:
  7.2 116.1 %all-reduce.3.cloned.1.call-start = ((), (), s32[]{:S(2)}) async-start(), calls=%async_computation | async-start | bytes 4194304 | tf_op jit(solution)/shard_map/psum | solution.py:34
  22.1 0.7 copy-start.3
  22.2 230.3 %all-reduce.5.cloned.1.call-start = ((), (), s32[]{:S(2)}) async-start(), calls=%async_computation.1 | async-start | bytes 4194304 | tf_op jit(solution)/shard_map/psum | solution.py:39
  125.1 1.4 copy-start
  125.1 17.6 %slice-start = ((s8[6291456]{0:T(1024)(128)(4,1)}), s8[4194304]{0:T(1024)(128)(4,1)S(1)}, s32[]{:S(2)}) async-start(s8[6291456]{0:T(1024)(128)(4,1)} %bitcast.83), calls=%async_computation.2 | async-start | bytes 8388608
  126.5 16.2 %slice-start.1 = ((s8[6291456]{0:T(1024)(128)(4,1)}), s8[2097152]{0:T(1024)(128)(4,1)S(1)}, s32[]{:S(2)}) async-start(s8[6291456]{0:T(1024)(128)(4,1)} %bitcast.83), calls=%async_computation.3 | async-start | bytes 4194304
  154.7 31.4 %copy-start.4 = (f32[2,128]{1,0:T(2,128)S(1)}, f32[2,128]{1,0:T(2,128)}, u32[]{:S(2)}) copy-start(f32[2,128]{1,0:T(2,128)} %param.9) | copy-start | bytes 3076
  186.1 68.3 %copy-start.2 = (f32[2,128]{1,0:T(2,128)}, f32[2,128]{1,0:T(2,128)S(1)}, u32[]{:S(2)}) copy-start(f32[2,128]{1,0:T(2,128)S(1)} %psum.23) | copy-start | bytes 3076
  254.4 1.4 copy-start.1
Sparse Core Ops, SparseCore 0:
  22.3 100.8 all-reduce.2
  154.9 97.5 all-reduce.4
where the time goes:
time: 279 us
  waiting for transfers between devices  167 us (60%)
  matrix products  55.9 us (20%)
  blocking collectives  31.1 us (11%)
  between operations  14.2 us (5%)
  other arithmetic  8.56 us (3%)
    psum x1, waiting for transfers between devices, on_device(): first_total = lax.psum(first, 'ga')  100 us
    psum x1, waiting for transfers between devices, on_device(): second_total, dot_new = lax.psum((second, local_dot), 'ga')  66.3 us
    dot_general x2, matrix products, correction(): jnp.einsum('pchnb,hng->pcbg', coefficient, occ_rows, precision=highest)  32.6 us
    psum x1, blocking collectives, on_device(): second_total, dot_new = lax.psum((second, local_dot), 'ga')  31.1 us
    dot_general x2, matrix products, margins(): jnp.einsum('hng,pcbg->phcnb', occupied, vectors, precision=highest)  23.3 us
  transfers between devices with their start and end apart: 2, of which 2 were waited for; matrix products, arithmetic and copies ran while one was open for 0% of the time, Pallas kernels for 0%

commit v1 on v0

--- a/solution.py
+++ b/solution.py
@@ -31,7 +31,11 @@
 def on_device(occupied, residual, old_direction, kin_ratio, old_dot):
     factor = teter_factor(kin_ratio)
     first = margins(occupied, residual)
-    first_total = lax.psum(first, "ga")
+
+    def rest_heaps_by_axis(my_tile, bus_axis):
+        return lax.all_gather(my_tile, axis_name=bus_axis).sum(axis=0)
+
+    first_total = rest_heaps_by_axis(first, "ga")
     gradient = residual - correction(first_total, occupied)
     precond = factor * gradient
     local_dot = jnp.sum(factor * (gradient[:, 0] ** 2 + gradient[:, 1] ** 2), axis=-1)

time: 279 us -> 360 us (1.29)
  waiting for transfers between devices: 167 us -> 235 us
  other arithmetic: 8.56 us -> 18.9 us
    all_gather x0 -> x1, waiting for transfers between devices: none -> 170 us  [rest_heaps_by_axis(): return lax.all_gather(my_tile, axis_name=bus_axis).sum(axis=0)]
    psum x1 -> x0, waiting for transfers between devices: 100 us -> none  [on_device(): first_total = lax.psum(first, 'ga')]
    reduce_sum x0 -> x1, other arithmetic: none -> 12.1 us  [rest_heaps_by_axis(): return lax.all_gather(my_tile, axis_name=bus_axis).sum(axis=0)]
where the time goes in v1:
time: 360 us
  waiting for transfers between devices  235 us (65%)
  matrix products  55.9 us (16%)
  blocking collectives  33.1 us (9%)
  other arithmetic  18.9 us (5%)
  between operations  14.2 us (4%)
    all_gather x1, waiting for transfers between devices, rest_heaps_by_axis(): return lax.all_gather(my_tile, axis_name=bus_axis).sum(axis=0)  170 us
    psum x1, waiting for transfers between devices, on_device(): second_total, dot_new = lax.psum((second, local_dot), 'ga')  65 us
    psum x1, blocking collectives, on_device(): second_total, dot_new = lax.psum((second, local_dot), 'ga')  33.1 us
    dot_general x2, matrix products, correction(): jnp.einsum('pchnb,hng->pcbg', coefficient, occ_rows, precision=highest)  32.6 us
    dot_general x2, matrix products, margins(): jnp.einsum('hng,pcbg->phcnb', occupied, vectors, precision=highest)  23.3 us
    reduce_sum x1, other arithmetic, rest_heaps_by_axis(): return lax.all_gather(my_tile, axis_name=bus_axis).sum(axis=0)  12.1 us
  transfers between devices with their start and end apart: 2, of which 2 were waited for; matrix products, arithmetic and copies ran while one was open for 0% of the time, Pallas kernels for 0%

profile of v1, /device:TPU:0, one launch (start us, length us, event | category | flops | bytes accessed | tf_op | source)
XLA Modules:
  0.0 360.1 jit_solution(5662769204827494497)
XLA Ops:
  7.2 13.1 %fusion.12 = f32[2,2,2,1024,128]{3,4,1,2,0:T(8,128)S(1)} fusion(f32[2,1024,768]{2,1,0:T(8,128)} %param.5, f32[2,2,128,768]{3,2,1,0:T(8,128)} %param.6), kind=kOutput, calls=%fused_computation.13 | convolution fusion | flops 9663676416 | bytes 12058624 | tf_op jit(solution)/shard_map/hng,pcbg->phcnb/dot_general | solution.py:15
  20.4 0.2 fusion.33
  20.5 0.2 fusion.35
  20.7 1.5 pad_maximum_fusion.1
  22.2 0.2 all-reduce.2.cloned.1.call-start
  22.4 0.4 copy-done.3
  22.9 170.3 %all-gather.3.cloned.1.call-done = f32[32,2,1024,128]{2,3,0,1:T(8,128)} async-done(((f32[2,2,1024,128]{2,3,0,1:T(8,128)}), f32[32,2,1024,128]{2,3,0,1:T(8,128)}) %all-gather.3.cloned.1.call-update) | async-done | bytes 33554448 | tf_op jit(solution)/shard_map/all_gather | solution.py:36
  193.1 12.1 %reduce_sum.18 = f32[2,2,1024,128]{2,3,0,1:T(8,128)S(1)} reduce(f32[16,2,2,1024,128]{3,4,1,0,2:T(8,128)} %bitcast.94, f32[]{:T(128)} %constant.5.clone.1), dimensions={0}, to_apply=%region_0.0 | reduce | flops 7864320 | bytes 35651588 | tf_op jit(solution)/shard_map/reduce_sum | solution.py:36
  205.2 0.2 slice_bitcast_fusion.2
  205.5 0.1 fusion.46
  205.6 0.6 maximum_bitcast_fusion
  206.2 0.8 copy-done
  207.0 16.2 %bitcast_subtract_fusion.1 = f32[2,2,128,768]{3,2,1,0:T(8,128)S(1)} fusion(f32[2,2,128,768]{3,2,1,0:T(8,128)S(1)} %copy-done, f32[2,1024,768]{2,1,0:T(8,128)} %param.5, f32[2,1,2,1024,128]{3,4,2,1,0:T(8,128)S(1)} %get-tuple-element.10, f32[2,1,2,1024,128]{3,4,2,1,0:T(8,128)S(1)} %get-tuple-element.9), kind=kOutput, calls=%fused_computation.25 | convolution fusion | flops 9665118208 | bytes 13631488 | tf_op jit(solution)/shard_map/pchnb,hng->pcbg/dot_general | solution.py:28
  223.2 10.2 %fusion.15 = f32[2,2,2,1024,128]{3,4,1,2,0:T(8,128)S(1)} fusion(f32[2,1024,768]{2,1,0:T(8,128)S(1)} %bitcast.93, f32[2,2,128,768]{3,2,1,0:T(8,128)S(1)} %bitcast_subtract_fusion.1, f32[768]{0:T(1024)S(1)} %add_divide_fusion), kind=kOutput, calls=%fused_computation.14 | convolution fusion | flops 9664069632 | bytes 12061696 | tf_op jit(solution)/shard_map/hng,pcbg->phcnb/dot_general | solution.py:15
  233.4 0.2 fusion.30
  233.6 0.2 fusion.32
  233.7 1.4 pad_maximum_fusion.2
  235.2 0.2 fusion.39
  235.4 33.1 %psum.15 = f32[2,128]{1,0:T(2,128)S(1)} all-reduce(f32[2,128]{1,0:T(2,128)S(1)} %fusion.39), channel_id=1, replica_groups=mesh['groups'=2,'ga'=16] {'ga'}, use_global_device_ids=true, to_apply=%region_3.0 | all-reduce | flops 256 | bytes 2048 | tf_op jit(solution)/shard_map/psum | solution.py:43
  268.5 65.0 %all-reduce.2.cloned.1.call-done = f32[2,2,1024,128]{2,3,0,1:T(8,128)} async-done(((f32[2,2,1024,128]{2,3,0,1:T(8,128)}), f32[2,2,1024,128]{2,3,0,1:T(8,128)}) %all-reduce.2.cloned.1.call-update) | async-done | bytes 2097168 | tf_op jit(solution)/shard_map/psum | solution.py:43
  333.5 1.9 slice_negate_fusion
  335.4 0.5 maximum_bitcast_fusion.2
  335.9 0.9 copy-done.1
  336.8 16.4 %fusion.20 = f32[2,2,128,768]{3,2,1,0:T(8,128)} fusion(f32[2,2,128,768]{3,2,1,0:T(8,128)S(1)} %copy-done.1, f32[2,1024,768]{2,1,0:T(8,128)} %param.5, f32[2,2,128,768]{3,2,1,0:T(8,128)S(1)} %bitcast_subtract_fusion.1, f32[2,128]{1,0:T(2,128)S(1)} %div.7, f32[768]{0:T(1024)S(1)} %add_divide_fusion, f32[2,1,2,1024,128]{3,4,0,2,1:T(8,128)S(1)} %get-tuple-element.8, ...), kind=kOutput, calls=%fused_computation.24 | convolution fusion | flops 9666297856 | bytes 15208448 | tf_op jit(solution)/shard_map/pchnb,hng->pcbg/dot_general | solution.py:28
  (17 shorter events, 0.1 us)
Async XLA Ops:
  7.2 186.0 %all-gather.3.cloned.1.call-start = ((), (), s32[]{:S(2)}) async-start(), calls=%async_computation.1 | async-start | bytes 35651584 | tf_op jit(solution)/shard_map/all_gather | solution.py:36
  22.2 0.7 copy-start.3
  22.2 311.3 %all-reduce.2.cloned.1.call-start = ((), (), s32[]{:S(2)}) async-start(), calls=%async_computation | async-start | bytes 4194304 | tf_op jit(solution)/shard_map/psum | solution.py:43
  205.6 1.4 copy-start
  205.6 17.6 %slice-start = ((s8[6291456]{0:T(1024)(128)(4,1)}), s8[4194304]{0:T(1024)(128)(4,1)S(1)}, s32[]{:S(2)}) async-start(s8[6291456]{0:T(1024)(128)(4,1)} %bitcast.92), calls=%async_computation.2 | async-start | bytes 8388608
  207.0 16.2 %slice-start.1 = ((s8[6291456]{0:T(1024)(128)(4,1)}), s8[2097152]{0:T(1024)(128)(4,1)S(1)}, s32[]{:S(2)}) async-start(s8[6291456]{0:T(1024)(128)(4,1)} %bitcast.92), calls=%async_computation.3 | async-start | bytes 4194304
  235.2 33.3 %copy-start.4 = (f32[2,128]{1,0:T(2,128)S(1)}, f32[2,128]{1,0:T(2,128)}, u32[]{:S(2)}) copy-start(f32[2,128]{1,0:T(2,128)} %param.9) | copy-start | bytes 3076
  268.5 66.9 %copy-start.2 = (f32[2,128]{1,0:T(2,128)}, f32[2,128]{1,0:T(2,128)S(1)}, u32[]{:S(2)}) copy-start(f32[2,128]{1,0:T(2,128)S(1)} %psum.15) | copy-start | bytes 3076
  335.4 1.4 copy-start.1
Sparse Core Ops, SparseCore 0:
  22.3 170.7 all-gather.2
  235.3 98.1 all-reduce.1
